TPU v7x, 128 devices: a whole 4x4x4 slice. The times are simulated.
128 devices in a mesh: sample: 4 (over x), gz: 32 (over z, y, core).
Axes of the slice: x: 4, y: 4, z: 4, core: 2. Of those that a mesh axis runs over, the one named last changes fastest.
Arguments:
- field_now: float32 [12, 64, 160, 256], P('sample', 'gz'), parts along dimension 0, may hold values from -6 to 6
- field_before: float32 [12, 64, 160, 256], P('sample', 'gz'), parts along dimension 0, may hold values from -6 to 6
- lame_lambda: float32 [64, 640, 256], P('gz', 'sample'), parts along dimension 1, may hold values from 0.5 to 1.5
- shear_modulus: float32 [64, 640, 256], P('gz', 'sample'), parts along dimension 1, may hold values from 0.5 to 1.5
- density: float32 [64, 640, 256], P('gz', 'sample'), parts along dimension 1, may hold values from 1 to 2
- source_field: float32 [12, 64, 160, 256], P('sample', 'gz'), parts along dimension 0, may hold values from -6 to 6
- wavelet: float32 [32], P('sample'), parts along dimension 0, may hold values from -4 to 4
- prior_mean: float32 [64, 640, 256], P('gz', 'sample'), parts along dimension 1, may hold values from 0.5 to 1.5
- steps_taken: float32 [16, 64, 160, 256], P('sample', 'gz'), parts along dimension 0
- grad_change: float32 [16, 64, 160, 256], P('sample', 'gz'), parts along dimension 0, as said below
Outputs:
- field_final: float32 [12, 64, 160, 256], P('sample', 'gz'), parts along dimension 0
- gradient: float32 [64, 640, 256], P('gz', 'sample'), parts along dimension 1
- direction: float32 [64, 640, 256], P('gz', 'sample'), parts along dimension 1
There are 4 independent parts, one for each index of `sample`. A program takes and returns all parts, laid end to end along the dimension named above; each array names one. Nothing has to cross between parts.
Inputs may be any that keep to these rules, and one draw needn't show every extreme that they name: Each entry of grad_change is 0.5 to 2 times the matching entry of steps_taken.
All inputs are finite; a program needn't handle non-finite values.
Results may differ from a plain program's by a relative error of at most 0.0003.
Values sent between devices are 32-bit elements; how exact they have to be, the bound alone decides.
A program may use at most 64 MiB of HBM per device.

v0:
```python
import jax
import jax.numpy as jnp
from jax import lax
from jax.experimental import pallas as pl
from jax.experimental.pallas import tpu as pltpu
from jax.sharding import PartitionSpec as P

STEPS = 8
PAIRS = 4
ROWS = 16
PAD = 8
LANES = 128
MESH = pl.DeviceIdType.MESH


def kernel(
    now, before, lame, shear, density, source, wavelet, prior, steps, changes,
    out_field, out_gradient, out_direction,
    field, halo, first_coef, second_coef, force, grad, s_vec, y_vec, spare, row, rows,
    send_sem, recv_sem, load_sem, store_sem, sum_send, sum_recv,
):
    me = lax.axis_index("gz")
    count = lax.axis_size("gz")
    nx = first_coef.shape[2]
    chunks = nx // ROWS
    padded = nx + 2 * PAD
    zero = jnp.zeros((8, LANES), jnp.float32)
    lane = lax.broadcasted_iota(jnp.int32, (8, LANES), 1)
    row_lane = lax.broadcasted_iota(jnp.int32, (1, LANES), 1)
    at_start = lane == 0
    at_end = lane == LANES - 1
    exists = (me > 0, me < count - 1)
    beside = (jnp.maximum(me - 1, 0), jnp.minimum(me + 1, count - 1))

    inner = pl.ds(PAD, nx)
    loads = []

    def load(src, dst_of):
        for h in range(2):
            copy = pltpu.make_async_copy(
                src.at[..., pl.ds(h * LANES, LANES)], dst_of(h), load_sem.at[len(loads)]
            )
            copy.start()
            loads.append(copy)

    load(now, lambda h: field.at[0, :, :, h, inner, :])
    load(lame, lambda h: first_coef.at[:, h])
    load(shear, lambda h: second_coef.at[:, h])
    load(density, lambda h: spare.at[:, h])
    load(source, lambda h: force.at[:, :, h])
    load(prior, lambda h: grad.at[:, h])
    load(before, lambda h: field.at[1, :, :, h, inner, :])
    load(steps, lambda h: s_vec.at[:, :, h])
    load(changes, lambda h: y_vec.at[:, :, h])

    barrier = pltpu.get_barrier_semaphore()

    def greet(k, carry):
        pl.semaphore_signal(
            barrier, inc=1, device_id={"gz": lax.rem(me + k, count)}, device_id_type=MESH
        )
        return carry

    for par in range(2):
        for c in range(3):
            for d in range(2):
                for h in range(2):
                    for edge in (0, padded - PAD):
                        field[par, c, d, h, edge : edge + 8, :] = zero
                        halo[par, d, c, h, edge : edge + 8, :] = zero
    for d in range(2):

        @pl.when(jnp.logical_not(exists[d]))
        def _():
            def clear(i, carry):
                at = pl.ds(pl.multiple_of(i * 8, 8), 8)
                for par in range(2):
                    for c in range(3):
                        for h in range(2):
                            halo[par, d, c, h, at, :] = zero
                return carry

            lax.fori_loop(0, padded // 8, clear, 0)

    lax.fori_loop(1, count, greet, 0)
    pl.semaphore_wait(barrier, count - 1)

    def outgoing(par, d, j):
        at = pl.ds(pl.multiple_of(PAD + j * ROWS, 8), ROWS)
        return pltpu.make_async_remote_copy(
            src_ref=field.at[par, :, d, :, at, :],
            dst_ref=halo.at[par, 1 - d, :, :, at, :],
            send_sem=send_sem.at[par, d, j],
            recv_sem=recv_sem.at[par, 1 - d, j],
            device_id={"gz": beside[d]},
            device_id_type=MESH,
        )

    def incoming(par, d, j):
        at = pl.ds(pl.multiple_of(PAD + j * ROWS, 8), ROWS)
        return pltpu.make_async_remote_copy(
            src_ref=field.at[par, :, d, :, at, :],
            dst_ref=halo.at[par, d, :, :, at, :],
            send_sem=send_sem.at[par, d, j],
            recv_sem=recv_sem.at[par, d, j],
            device_id={"gz": beside[d]},
            device_id_type=MESH,
        )

    def send(par, j):
        for d in range(2):
            pl.when(exists[d])(lambda d=d: outgoing(par, d, j).start())

    def wait_sent(par, j):
        for d in range(2):
            pl.when(exists[d])(lambda d=d: outgoing(par, d, j).wait_send())

    def wait_halo(par, j):
        for d in range(2):
            pl.when(exists[d])(lambda d=d: incoming(par, d, j).wait_recv())

    for copy in loads[:2]:
        copy.wait()

    def first_send(j, carry):
        send(0, j)
        return carry

    lax.fori_loop(0, chunks, first_send, 0)

    for copy in loads[2:12]:
        copy.wait()

    def prepare(i, carry):
        at = pl.ds(pl.multiple_of(i * 8, 8), 8)
        for p in range(2):
            for h in range(2):
                mu = second_coef[p, h, at, :]
                coeff = 0.04 / spare[p, h, at, :]
                first_coef[p, h, at, :] = 0.25 * coeff * (first_coef[p, h, at, :] + mu)
                second_coef[p, h, at, :] = coeff * mu
                grad[p, h, at, :] = mu - grad[p, h, at, :]
                for c in range(3):
                    force[c, p, h, at, :] = coeff * force[c, p, h, at, :]
        return carry

    lax.fori_loop(0, nx // 8, prepare, 0)

    for copy in loads[12:]:
        copy.wait()
    wanted = [("sy", i, j) for i in range(PAIRS) for j in range(i, PAIRS)]
    wanted += [("yy", i, j) for i in range(PAIRS) for j in range(i, PAIRS)]

    def gram(i, sums):
        at = pl.ds(pl.multiple_of(i * 8, 8), 8)
        sums = list(sums)
        for p in range(2):
            for h in range(2):
                s = [s_vec[k, p, h, at, :] for k in range(PAIRS)]
                y = [y_vec[k, p, h, at, :] for k in range(PAIRS)]
                for w, (kind, a, b) in enumerate(wanted):
                    sums[w] = sums[w] + (s[a] if kind == "sy" else y[a]) * y[b]
        return tuple(sums)

    def total_of(x):
        return jnp.sum(jnp.sum(x, axis=0, keepdims=True), axis=1, keepdims=True)

    sums = lax.fori_loop(0, nx // 8, gram, (zero,) * len(wanted))
    gram_row = jnp.zeros((1, LANES), jnp.float32)
    for w, x in enumerate(sums):
        gram_row = jnp.where(row_lane == 2 * PAIRS + w, total_of(x), gram_row)
    row[...] = gram_row

    def along_y(v):
        back = [pltpu.roll(x, 1, 1) for x in v]
        ahead = [pltpu.roll(x, LANES - 1, 1) for x in v]
        plus = (jnp.where(at_end, ahead[1], ahead[0]), jnp.where(at_end, 0.0, ahead[1]))
        minus = (jnp.where(at_start, 0.0, back[0]), jnp.where(at_start, back[0], back[1]))
        return plus, minus

    def add(a, b):
        return (a[0] + b[0], a[1] + b[1])

    def sub(a, b):
        return (a[0] - b[0], a[1] - b[1])

    def block(cur, nxt, amplitude, base):
        at = pl.ds(base, 8)

        def rows_of(c, z, offset):
            from_row = pl.ds(base + PAD + offset, 8)
            if z in (-1, 2):
                return tuple(halo[cur, 0 if z < 0 else 1, c, h, from_row, :] for h in range(2))
            return tuple(field[cur, c, z, h, from_row, :] for h in range(2))

        u = {(c, z): rows_of(c, z, 0) for c in range(3) for z in (-1, 0, 1, 2)}
        up = {}
        down = {}
        for c in range(3):
            for z in (-1, 0, 1, 2) if c < 2 else (0, 1):
                up[c, z] = rows_of(c, z, 1)
                down[c, z] = rows_of(c, z, -1)
        dx = {key: sub(up[key], down[key]) for key in up}
        dy2 = {}
        sy = {}
        for z in (-1, 0, 1, 2):
            plus, minus = along_y(u[2, z])
            dy2[z] = sub(plus, minus)
            if z in (0, 1):
                sy[2, z] = add(plus, minus)
        mix0 = {z: add(dx[1, z], dy2[z]) for z in (-1, 0, 1, 2)}
        grads = []
        for z in range(2):
            for c in range(2):
                sy[c, z] = add(*along_y(u[c, z]))
            dz0 = sub(u[0, z + 1], u[0, z - 1])
            cross = [
                sub(mix0[z + 1], mix0[z - 1]),
                add(sub(dx[0, z + 1], dx[0, z - 1]), sub(*along_y(dx[2, z]))),
                sub(*along_y(add(dz0, dx[1, z]))),
            ]
            work = [None, None]
            for c in range(3):
                sz = add(u[c, z + 1], u[c, z - 1])
                sx = add(up[c, z], down[c, z])
                own = (sz, sx, sy[c, z])[c]
                for h in range(2):
                    centre = u[c, z][h]
                    twice = centre + centre
                    laplace = sz[h] + sx[h] + sy[c, z][h] - 6.0 * centre
                    div = 4.0 * (own[h] - twice) + cross[c][h]
                    field[nxt, c, z, h, pl.ds(base + PAD, 8), :] = (
                        twice
                        - field[nxt, c, z, h, pl.ds(base + PAD, 8), :]
                        + first_coef[z, h, at, :] * div
                        + second_coef[z, h, at, :] * laplace
                        + amplitude * force[c, z, h, at, :]
                    )
                    term = centre * laplace
                    work[h] = term if work[h] is None else work[h] + term
            for h in range(2):
                new = grad[z, h, at, :] + 0.02 * work[h]
                grad[z, h, at, :] = new
                grads.append((z, h, new))
        return grads

    def step(n, carry):
        cur = lax.rem(n, 2)
        nxt = 1 - cur
        amplitude = wavelet[n]
        wait_halo(cur, 0)

        def chunk(j, inside):
            pl.when(j + 1 < chunks)(lambda: wait_halo(cur, j + 1))
            pl.when(n >= 1)(lambda: wait_sent(nxt, j))
            for b in range(ROWS // 8):
                block(cur, nxt, amplitude, pl.multiple_of(j * ROWS + b * 8, 8))
            send(nxt, j)
            return inside

        return lax.fori_loop(0, chunks, chunk, carry)

    lax.fori_loop(0, STEPS - 1, step, 0)

    cur, nxt = (STEPS - 1) % 2, STEPS % 2
    wait_halo(cur, 0)

    def last_chunk(j, sums):
        pl.when(j + 1 < chunks)(lambda: wait_halo(cur, j + 1))
        wait_sent(nxt, j)
        sums = list(sums)
        for b in range(ROWS // 8):
            base = pl.multiple_of(j * ROWS + b * 8, 8)
            for z, h, g in block(cur, nxt, wavelet[STEPS - 1], base):
                for k in range(PAIRS):
                    sums[k] = sums[k] + s_vec[k, z, h, pl.ds(base, 8), :] * g
                    sums[PAIRS + k] = sums[PAIRS + k] + y_vec[k, z, h, pl.ds(base, 8), :] * g
        return tuple(sums)

    sums = lax.fori_loop(0, chunks, last_chunk, (zero,) * (2 * PAIRS))

    mine = row[...]
    for w, x in enumerate(sums):
        mine = jnp.where(row_lane == w, total_of(x), mine)
    row[...] = mine

    def tell(k, carry):
        pltpu.make_async_remote_copy(
            src_ref=row,
            dst_ref=rows.at[k - 1],
            send_sem=sum_send.at[0],
            recv_sem=sum_recv.at[0],
            device_id={"gz": lax.rem(me + k, count)},
            device_id_type=MESH,
        ).start()
        return carry

    lax.fori_loop(1, count, tell, 0)

    stores = []
    for h in range(2):
        half = pl.ds(h * LANES, LANES)
        stores.append(
            pltpu.make_async_copy(
                field.at[nxt, :, :, h, inner, :], out_field.at[..., half], store_sem.at[h]
            )
        )
        stores.append(
            pltpu.make_async_copy(grad.at[:, h], out_gradient.at[..., half], store_sem.at[2 + h])
        )
    for copy in stores:
        copy.start()

    def last_sent(j, carry):
        wait_sent(cur, j)
        return carry

    lax.fori_loop(0, chunks, last_sent, 0)

    everyone = pltpu.make_async_remote_copy(
        src_ref=rows,
        dst_ref=rows,
        send_sem=sum_send.at[0],
        recv_sem=sum_recv.at[0],
        device_id={"gz": lax.rem(me + 1, count)},
        device_id_type=MESH,
    )
    everyone.wait_send()
    everyone.wait_recv()
    total = row[...] + jnp.sum(rows[...], axis=0)

    def value(k):
        return jnp.sum(jnp.where(row_lane == k, total, 0.0), axis=1, keepdims=True)

    sg = [value(k) for k in range(PAIRS)]
    yg = [value(PAIRS + k) for k in range(PAIRS)]
    pair = {}
    for w, (kind, a, b) in enumerate(wanted):
        pair[kind, a, b] = value(2 * PAIRS + w)
        if kind == "yy":
            pair[kind, b, a] = pair[kind, a, b]
    alphas = [None] * PAIRS
    for i in reversed(range(PAIRS)):
        dot = sg[i]
        for j in range(i + 1, PAIRS):
            dot = dot - alphas[j] * pair["sy", i, j]
        alphas[i] = dot / pair["sy", i, i]
    gamma = pair["sy", PAIRS - 1, PAIRS - 1] / pair["yy", PAIRS - 1, PAIRS - 1]
    extra = []
    for i in range(PAIRS):
        dot = yg[i]
        for j in range(PAIRS):
            dot = dot - alphas[j] * pair["yy", i, j]
        dot = gamma * dot
        for j in range(i):
            dot = dot + extra[j] * pair["sy", j, i]
        extra.append(alphas[i] - dot / pair["sy", i, i])

    def wide(x):
        return jnp.broadcast_to(x, (8, LANES))

    of_g = wide(-gamma)
    of_y = [wide(gamma * alphas[i]) for i in range(PAIRS)]
    of_s = [wide(-extra[i]) for i in range(PAIRS)]

    def combine(i, carry):
        at = pl.ds(pl.multiple_of(i * 8, 8), 8)
        for p in range(2):
            for h in range(2):
                out = of_g * grad[p, h, at, :]
                for k in range(PAIRS):
                    out = out + of_y[k] * y_vec[k, p, h, at, :] + of_s[k] * s_vec[k, p, h, at, :]
                spare[p, h, at, :] = out
        return carry

    lax.fori_loop(0, nx // 8, combine, 0)
    for h in range(2):
        copy = pltpu.make_async_copy(
            spare.at[:, h], out_direction.at[..., pl.ds(h * LANES, LANES)], store_sem.at[4 + h]
        )
        copy.start()
        stores.append(copy)
    for copy in stores:
        copy.wait()


def on_device(*args):
    now = args[0]
    lame = args[2]
    nx = now.shape[2]
    count = lax.axis_size("gz")
    padded = nx + 2 * PAD
    chunks = nx // ROWS
    f32 = jnp.float32
    anywhere = pl.BlockSpec(memory_space=pl.ANY)
    in_specs = [anywhere] * 10
    in_specs[6] = pl.BlockSpec(memory_space=pltpu.SMEM)
    plane = (2, 2, nx, LANES)
    return pl.pallas_call(
        kernel,
        out_shape=(
            jax.ShapeDtypeStruct(now.shape, f32),
            jax.ShapeDtypeStruct(lame.shape, f32),
            jax.ShapeDtypeStruct(lame.shape, f32),
        ),
        in_specs=in_specs,
        out_specs=(anywhere,) * 3,
        scratch_shapes=[
            pltpu.VMEM((2, 3, 2, 2, padded, LANES), f32),
            pltpu.VMEM((2, 2, 3, 2, padded, LANES), f32),
            pltpu.VMEM(plane, f32),
            pltpu.VMEM(plane, f32),
            pltpu.VMEM((3, *plane), f32),
            pltpu.VMEM(plane, f32),
            pltpu.VMEM((PAIRS, *plane), f32),
            pltpu.VMEM((PAIRS, *plane), f32),
            pltpu.VMEM(plane, f32),
            pltpu.VMEM((1, LANES), f32),
            pltpu.VMEM((count - 1, 1, LANES), f32),
            pltpu.SemaphoreType.DMA((2, 2, chunks)),
            pltpu.SemaphoreType.DMA((2, 2, chunks)),
            pltpu.SemaphoreType.DMA((18,)),
            pltpu.SemaphoreType.DMA((6,)),
            pltpu.SemaphoreType.DMA((1,)),
            pltpu.SemaphoreType.DMA((1,)),
        ],
        compiler_params=pltpu.CompilerParams(
            collective_id=0, has_side_effects=True, vmem_limit_bytes=60 * 1024 * 1024
        ),
        name="leapfrog",
    )(*args)


def solution(mesh):
    placed = (
        P("sample", "gz", None, None),
        P("sample", "gz", None, None),
        P("gz", "sample", None),
        P("gz", "sample", None),
        P("gz", "sample", None),
        P("sample", "gz", None, None),
        P("sample"),
        P("gz", "sample", None),
        P("sample", "gz", None, None),
        P("sample", "gz", None, None),
    )
    return jax.shard_map(
        on_device,
        mesh=mesh,
        in_specs=placed,
        out_specs=(P("sample", "gz", None, None), P("gz", "sample", None), P("gz", "sample", None)),
        check_vma=False,
    )
```

profile of v0, /device:TPU:1, one launch (start us, length us, event | category | flops | bytes accessed | tf_op | source)
XLA Modules:
  0.0 64.7 jit_solution(16810189211466735882)
XLA Ops:
  0.6 60.2 %leapfrog.1 = (f32[3,2,160,256]{3,2,1,0:T(8,128)}, f32[2,160,256]{2,1,0:T(8,128)}, f32[2,160,256]{2,1,0:T(8,128)}) custom-call(f32[3,2,160,256]{3,2,1,0:T(8,128)} %now.1, f32[3,2,160,256]{3,2,1,0:T(8,128)} %before.1, f32[2,160,256]{2,1,0:T(8,128)} %lame.1, f32[2,160,256]{2,1,0:T(8,128)} %shear.1, f32[2,160,256]{2,1,0:T(8,128)} %density.1, ...), custom_call_target="tpu_custom_call" | custom-call | tf_op jit(solution)/shard_map/leapfrog/pallas_call | solution.py:399
  60.9 0.0 copy-start.1
  60.9 0.0 copy-start
  60.9 2.3 %copy.16 = f32[3,2,160,256]{3,2,1,0:T(8,128)} copy(f32[3,2,160,256]{3,2,1,0:T(8,128)} %get-tuple-element.6) | data formatting | bytes 1966080
  63.2 0.0 copy-done.1
  63.2 0.7 %copy.17 = f32[2,160,256]{2,1,0:T(8,128)} copy(f32[2,160,256]{2,1,0:T(8,128)S(1)} %copy-done.1) | data formatting | bytes 655360
  63.9 0.0 copy-done
  63.9 0.7 %copy.18 = f32[2,160,256]{2,1,0:T(8,128)} copy(f32[2,160,256]{2,1,0:T(8,128)S(1)} %copy-done) | data formatting | bytes 655360
Async XLA Ops:
  60.9 2.3 %copy-start.1 = (f32[2,160,256]{2,1,0:T(8,128)S(1)}, f32[2,160,256]{2,1,0:T(8,128)}, u32[]{:S(2)}) copy-start(f32[2,160,256]{2,1,0:T(8,128)} %get-tuple-element.7) | copy-start | bytes 983044
  60.9 3.1 %copy-start = (f32[2,160,256]{2,1,0:T(8,128)S(1)}, f32[2,160,256]{2,1,0:T(8,128)}, u32[]{:S(2)}) copy-start(f32[2,160,256]{2,1,0:T(8,128)} %get-tuple-element.8) | copy-start | bytes 983044
where the time goes:
time: 64.8 us; the launch traced here: 64.7 us
  Pallas kernels  60.2 us (93%)
  local copies, waits for them, and re-layouts  3.78 us (6%)
  between operations  0.66 us (1%)
    pallas_call x1, Pallas kernels, on_device(): pl.pallas_call(kernel, out_shape=(jax.ShapeDtypeStruct(now.shape, f32), j...  60.2 us
    unnamed x7, local copies, waits for them, and re-layouts  3.78 us

commit v1 on v0

--- a/solution.py
+++ b/solution.py
@@ -14,10 +14,10 @@
 
 
 def kernel(
-    now, before, lame, shear, density, source, wavelet, prior, steps, changes,
-    out_field, out_gradient, out_direction,
-    field, halo, first_coef, second_coef, force, grad, s_vec, y_vec, spare, row, rows,
-    send_sem, recv_sem, load_sem, store_sem, sum_send, sum_recv,
+    now, before, lame, shear, density, source, wave, prior, steps, changes,
+    final, grad, spare,
+    wavelet, field, halo, first_coef, second_coef, force, s_vec, y_vec, row, rows,
+    send_sem, recv_sem, load_sem, hello_sem, sum_send, sum_recv,
 ):
     me = lax.axis_index("gz")
     count = lax.axis_size("gz")
@@ -44,6 +44,8 @@
             loads.append(copy)
 
     load(now, lambda h: field.at[0, :, :, h, inner, :])
+    wave_copy = pltpu.make_async_copy(wave, wavelet, load_sem.at[18])
+    wave_copy.start()
     load(lame, lambda h: first_coef.at[:, h])
     load(shear, lambda h: second_coef.at[:, h])
     load(density, lambda h: spare.at[:, h])
@@ -54,12 +56,11 @@
     load(changes, lambda h: y_vec.at[:, :, h])
 
     barrier = pltpu.get_barrier_semaphore()
-
-    def greet(k, carry):
-        pl.semaphore_signal(
-            barrier, inc=1, device_id={"gz": lax.rem(me + k, count)}, device_id_type=MESH
-        )
-        return carry
+    for d in range(2):
+
+        @pl.when(exists[d])
+        def _():
+            pl.semaphore_signal(barrier, inc=1, device_id={"gz": beside[d]}, device_id_type=MESH)
 
     for par in range(2):
         for c in range(3):
@@ -82,8 +83,7 @@
 
             lax.fori_loop(0, padded // 8, clear, 0)
 
-    lax.fori_loop(1, count, greet, 0)
-    pl.semaphore_wait(barrier, count - 1)
+    pl.semaphore_wait(barrier, jnp.where(me > 0, 1, 0) + jnp.where(me < count - 1, 1, 0))
 
     def outgoing(par, d, j):
         at = pl.ds(pl.multiple_of(PAD + j * ROWS, 8), ROWS)
@@ -119,6 +119,42 @@
         for d in range(2):
             pl.when(exists[d])(lambda d=d: incoming(par, d, j).wait_recv())
 
+    rounds = []
+    while 4 << len(rounds) < count:
+        rounds.append(4 << len(rounds))
+
+    def far(r, d):
+        return me + rounds[r] if d else me - rounds[r]
+
+    def within(r, d):
+        return far(r, d) < count if d else far(r, d) >= 0
+
+    def tell_far(r):
+        for d in range(2):
+
+            @pl.when(within(r, d))
+            def _():
+                pl.semaphore_signal(
+                    hello_sem.at[r, 1 - d], inc=1, device_id={"gz": far(r, d)}, device_id_type=MESH
+                )
+
+    def hear_far(r):
+        for d in range(2):
+
+            @pl.when(within(r, d))
+            def _():
+                pl.semaphore_wait(hello_sem.at[r, d], 1)
+
+    def acquaint(n):
+        for r in range(len(rounds) + 1):
+
+            @pl.when(n == 2 + r)
+            def _():
+                if r > 0:
+                    hear_far(r - 1)
+                if r < len(rounds):
+                    tell_far(r)
+
     for copy in loads[:2]:
         copy.wait()
 
@@ -128,6 +164,7 @@
 
     lax.fori_loop(0, chunks, first_send, 0)
 
+    wave_copy.wait()
     for copy in loads[2:12]:
         copy.wait()
 
@@ -184,7 +221,7 @@
     def sub(a, b):
         return (a[0] - b[0], a[1] - b[1])
 
-    def block(cur, nxt, amplitude, base):
+    def block(cur, nxt, amplitude, base, out=None):
         at = pl.ds(base, 8)
 
         def rows_of(c, z, offset):
@@ -229,13 +266,17 @@
                     twice = centre + centre
                     laplace = sz[h] + sx[h] + sy[c, z][h] - 6.0 * centre
                     div = 4.0 * (own[h] - twice) + cross[c][h]
-                    field[nxt, c, z, h, pl.ds(base + PAD, 8), :] = (
+                    new = (
                         twice
                         - field[nxt, c, z, h, pl.ds(base + PAD, 8), :]
                         + first_coef[z, h, at, :] * div
                         + second_coef[z, h, at, :] * laplace
                         + amplitude * force[c, z, h, at, :]
                     )
+                    if out is None:
+                        field[nxt, c, z, h, pl.ds(base + PAD, 8), :] = new
+                    else:
+                        out[c, z, h, at, :] = new
                     term = centre * laplace
                     work[h] = term if work[h] is None else work[h] + term
             for h in range(2):
@@ -249,6 +290,7 @@
         nxt = 1 - cur
         amplitude = wavelet[n]
         wait_halo(cur, 0)
+        acquaint(n)
 
         def chunk(j, inside):
             pl.when(j + 1 < chunks)(lambda: wait_halo(cur, j + 1))
@@ -267,11 +309,10 @@
 
     def last_chunk(j, sums):
         pl.when(j + 1 < chunks)(lambda: wait_halo(cur, j + 1))
-        wait_sent(nxt, j)
         sums = list(sums)
         for b in range(ROWS // 8):
             base = pl.multiple_of(j * ROWS + b * 8, 8)
-            for z, h, g in block(cur, nxt, wavelet[STEPS - 1], base):
+            for z, h, g in block(cur, nxt, wavelet[STEPS - 1], base, final):
                 for k in range(PAIRS):
                     sums[k] = sums[k] + s_vec[k, z, h, pl.ds(base, 8), :] * g
                     sums[PAIRS + k] = sums[PAIRS + k] + y_vec[k, z, h, pl.ds(base, 8), :] * g
@@ -284,34 +325,28 @@
         mine = jnp.where(row_lane == w, total_of(x), mine)
     row[...] = mine
 
-    def tell(k, carry):
+    spots = [(k,) for k in range(1, count)]
+    if count == 32:
+        spots = [(a, b, c) for a in range(4) for b in range(4) for c in range(2)][1:]
+        spots.sort(key=lambda t: -min(t[0], 4 - t[0]) - min(t[1], 4 - t[1]) - 0.1 * t[2])
+    core, along, slow = lax.rem(me, 2), lax.rem(me // 2, 4), me // 8
+    for k, spot in enumerate(spots):
+        if count == 32:
+            other = lax.rem(slow + spot[0], 4) * 8 + lax.rem(along + spot[1], 4) * 2
+            other = other + (1 - core if spot[2] else core)
+        else:
+            other = lax.rem(me + spot[0], count)
         pltpu.make_async_remote_copy(
             src_ref=row,
-            dst_ref=rows.at[k - 1],
+            dst_ref=rows.at[k],
             send_sem=sum_send.at[0],
             recv_sem=sum_recv.at[0],
-            device_id={"gz": lax.rem(me + k, count)},
+            device_id={"gz": other},
             device_id_type=MESH,
         ).start()
-        return carry
-
-    lax.fori_loop(1, count, tell, 0)
-
-    stores = []
-    for h in range(2):
-        half = pl.ds(h * LANES, LANES)
-        stores.append(
-            pltpu.make_async_copy(
-                field.at[nxt, :, :, h, inner, :], out_field.at[..., half], store_sem.at[h]
-            )
-        )
-        stores.append(
-            pltpu.make_async_copy(grad.at[:, h], out_gradient.at[..., half], store_sem.at[2 + h])
-        )
-    for copy in stores:
-        copy.start()
 
     def last_sent(j, carry):
+        wait_sent(nxt, j)
         wait_sent(cur, j)
         return carry
 
@@ -374,13 +409,23 @@
         return carry
 
     lax.fori_loop(0, nx // 8, combine, 0)
+
+
+def write_out(final, grad, spare, out_field, out_gradient, out_direction, sem):
+    copies = []
     for h in range(2):
-        copy = pltpu.make_async_copy(
-            spare.at[:, h], out_direction.at[..., pl.ds(h * LANES, LANES)], store_sem.at[4 + h]
-        )
+        half = pl.ds(h * LANES, LANES)
+        for src, dst in (
+            (final.at[:, :, h], out_field),
+            (grad.at[:, h], out_gradient),
+            (spare.at[:, h], out_direction),
+        ):
+            copies.append(
+                pltpu.make_async_copy(src, dst.at[..., half], sem.at[len(copies)])
+            )
+    for copy in copies:
         copy.start()
-        stores.append(copy)
-    for copy in stores:
+    for copy in copies:
         copy.wait()
 
 
@@ -392,43 +437,55 @@
     padded = nx + 2 * PAD
     chunks = nx // ROWS
     f32 = jnp.float32
-    anywhere = pl.BlockSpec(memory_space=pl.ANY)
-    in_specs = [anywhere] * 10
-    in_specs[6] = pl.BlockSpec(memory_space=pltpu.SMEM)
+    hbm = pl.BlockSpec(memory_space=pltpu.HBM)
+    vmem = pl.BlockSpec(memory_space=pltpu.VMEM)
+    in_specs = [hbm] * 10
     plane = (2, 2, nx, LANES)
+    halves = pl.pallas_call(
+        kernel,
+        out_shape=(
+            jax.ShapeDtypeStruct((3, *plane), f32),
+            jax.ShapeDtypeStruct(plane, f32),
+            jax.ShapeDtypeStruct(plane, f32),
+        ),
+        in_specs=in_specs,
+        out_specs=(vmem,) * 3,
+        scratch_shapes=[
+            pltpu.SMEM((STEPS,), f32),
+            pltpu.VMEM((2, 3, 2, 2, padded, LANES), f32),
+            pltpu.VMEM((2, 2, 3, 2, padded, LANES), f32),
+            pltpu.VMEM(plane, f32),
+            pltpu.VMEM(plane, f32),
+            pltpu.VMEM((3, *plane), f32),
+            pltpu.VMEM((PAIRS, *plane), f32),
+            pltpu.VMEM((PAIRS, *plane), f32),
+            pltpu.VMEM((1, LANES), f32),
+            pltpu.VMEM((count - 1, 1, LANES), f32),
+            pltpu.SemaphoreType.DMA((2, 2, chunks)),
+            pltpu.SemaphoreType.DMA((2, 2, chunks)),
+            pltpu.SemaphoreType.DMA((19,)),
+            pltpu.SemaphoreType.REGULAR((3, 2)),
+            pltpu.SemaphoreType.DMA((1,)),
+            pltpu.SemaphoreType.DMA((1,)),
+        ],
+        compiler_params=pltpu.CompilerParams(
+            collective_id=0, has_side_effects=True, vmem_limit_bytes=20 * 1024 * 1024
+        ),
+        name="leapfrog",
+    )(*[pltpu.with_memory_space_constraint(x, pltpu.HBM) for x in args])
     return pl.pallas_call(
-        kernel,
+        write_out,
         out_shape=(
             jax.ShapeDtypeStruct(now.shape, f32),
             jax.ShapeDtypeStruct(lame.shape, f32),
             jax.ShapeDtypeStruct(lame.shape, f32),
         ),
-        in_specs=in_specs,
-        out_specs=(anywhere,) * 3,
-        scratch_shapes=[
-            pltpu.VMEM((2, 3, 2, 2, padded, LANES), f32),
-            pltpu.VMEM((2, 2, 3, 2, padded, LANES), f32),
-            pltpu.VMEM(plane, f32),
-            pltpu.VMEM(plane, f32),
-            pltpu.VMEM((3, *plane), f32),
-            pltpu.VMEM(plane, f32),
-            pltpu.VMEM((PAIRS, *plane), f32),
-            pltpu.VMEM((PAIRS, *plane), f32),
-            pltpu.VMEM(plane, f32),
-            pltpu.VMEM((1, LANES), f32),
-            pltpu.VMEM((count - 1, 1, LANES), f32),
-            pltpu.SemaphoreType.DMA((2, 2, chunks)),
-            pltpu.SemaphoreType.DMA((2, 2, chunks)),
-            pltpu.SemaphoreType.DMA((18,)),
-            pltpu.SemaphoreType.DMA((6,)),
-            pltpu.SemaphoreType.DMA((1,)),
-            pltpu.SemaphoreType.DMA((1,)),
-        ],
-        compiler_params=pltpu.CompilerParams(
-            collective_id=0, has_side_effects=True, vmem_limit_bytes=60 * 1024 * 1024
-        ),
-        name="leapfrog",
-    )(*args)
+        in_specs=[vmem] * 3,
+        out_specs=(hbm,) * 3,
+        scratch_shapes=[pltpu.SemaphoreType.DMA((6,))],
+        compiler_params=pltpu.CompilerParams(vmem_limit_bytes=8 * 1024 * 1024),
+        name="write_out",
+    )(*halves)
 
 
 def solution(mesh):

time: 64.8 us -> 59.5 us (0.918)
  local copies, waits for them, and re-layouts: 3.78 us -> 0 us
  Pallas kernels: 60.2 us -> 58.8 us
    unnamed x7 -> x0, local copies, waits for them, and re-layouts: 3.78 us -> none
    pallas_call x1 -> x2, Pallas kernels: 60.2 us -> 58.8 us  [the longest x1 57.6 us: on_device(): pl.pallas_call(kernel, out_shape=(jax.ShapeDtypeStruct((3, *plane), f32),...]
where the time goes in v1:
time: 59.5 us; the launch traced here: 59.4 us
  Pallas kernels  58.8 us (99%)
  between operations  0.64 us (1%)
    pallas_call x1, Pallas kernels, on_device(): pl.pallas_call(kernel, out_shape=(jax.ShapeDtypeStruct((3, *plane), f32),...  57.6 us
    pallas_call x1, Pallas kernels, on_device(): pl.pallas_call(write_out, out_shape=(jax.ShapeDtypeStruct(now.shape, f32)...  1.21 us

profile of v1, /device:TPU:1, one launch (start us, length us, event | category | flops | bytes accessed | tf_op | source)
XLA Modules:
  0.0 59.4 jit_solution(3997002123371358670)
XLA Ops:
  0.6 57.6 %leapfrog.1 = (f32[3,2,2,160,128]{4,3,2,1,0:T(8,128)S(1)}, f32[2,2,160,128]{3,2,1,0:T(8,128)S(1)}, f32[2,2,160,128]{3,2,1,0:T(8,128)S(1)}) custom-call(f32[3,2,160,256]{3,2,1,0:T(8,128)} %now.1, f32[3,2,160,256]{3,2,1,0:T(8,128)} %before.1, f32[2,160,256]{2,1,0:T(8,128)} %lame.1, f32[2,160,256]{2,1,0:T(8,128)} %shear.1, f32[2,160,256]{2,1,0:T(8,128)} %density.1, ...), custom_call_target="tpu_custom_call" | custom-call | tf_op jit(solution)/shard_map/leapfrog/pallas_call | solution.py:444
  58.2 1.2 %write_out.1 = (f32[3,2,160,256]{3,2,1,0:T(8,128)}, f32[2,160,256]{2,1,0:T(8,128)}, f32[2,160,256]{2,1,0:T(8,128)}) custom-call(f32[3,2,2,160,128]{4,3,2,1,0:T(8,128)S(1)} %get-tuple-element.6.final, f32[2,2,160,128]{3,2,1,0:T(8,128)S(1)} %get-tuple-element.7.grad, f32[2,2,160,128]{3,2,1,0:T(8,128)S(1)} %get-tuple-element.8.spare), custom_call_target="tpu_custom_call" | custom-call | tf_op jit(solution)/shard_map/write_out/pallas_call | solution.py:476

commit v2 on v1

--- a/solution.py
+++ b/solution.py
@@ -7,6 +7,8 @@
 
 STEPS = 8
 PAIRS = 4
+WANTED = [("sy", i, j) for i in range(PAIRS) for j in range(i, PAIRS)]
+WANTED += [("yy", i, j) for i in range(PAIRS) for j in range(i, PAIRS)]
 ROWS = 16
 PAD = 8
 LANES = 128
@@ -15,8 +17,8 @@
 
 def kernel(
     now, before, lame, shear, density, source, wave, prior, steps, changes,
-    final, grad, spare,
-    wavelet, field, halo, first_coef, second_coef, force, s_vec, y_vec, row, rows,
+    final, grad, s_vec, y_vec, total,
+    wavelet, field, halo, first_coef, second_coef, force, spare, products, row, rows,
     send_sem, recv_sem, load_sem, hello_sem, sum_send, sum_recv,
 ):
     me = lax.axis_index("gz")
@@ -43,24 +45,14 @@
             copy.start()
             loads.append(copy)
 
-    load(now, lambda h: field.at[0, :, :, h, inner, :])
-    wave_copy = pltpu.make_async_copy(wave, wavelet, load_sem.at[18])
-    wave_copy.start()
-    load(lame, lambda h: first_coef.at[:, h])
-    load(shear, lambda h: second_coef.at[:, h])
-    load(density, lambda h: spare.at[:, h])
-    load(source, lambda h: force.at[:, :, h])
-    load(prior, lambda h: grad.at[:, h])
-    load(before, lambda h: field.at[1, :, :, h, inner, :])
-    load(steps, lambda h: s_vec.at[:, :, h])
-    load(changes, lambda h: y_vec.at[:, :, h])
-
     barrier = pltpu.get_barrier_semaphore()
     for d in range(2):
 
         @pl.when(exists[d])
         def _():
             pl.semaphore_signal(barrier, inc=1, device_id={"gz": beside[d]}, device_id_type=MESH)
+
+    load(now, lambda h: field.at[0, :, :, h, inner, :])
 
     for par in range(2):
         for c in range(3):
@@ -83,6 +75,16 @@
 
             lax.fori_loop(0, padded // 8, clear, 0)
 
+    for copy in loads:
+        copy.wait()
+    wave_copy = pltpu.make_async_copy(wave, wavelet, load_sem.at[18])
+    wave_copy.start()
+    load(lame, lambda h: first_coef.at[:, h])
+    load(shear, lambda h: second_coef.at[:, h])
+    load(density, lambda h: spare.at[:, h])
+    load(source, lambda h: force.at[:, :, h])
+    load(prior, lambda h: grad.at[:, h])
+    load(before, lambda h: field.at[1, :, :, h, inner, :])
     pl.semaphore_wait(barrier, jnp.where(me > 0, 1, 0) + jnp.where(me < count - 1, 1, 0))
 
     def outgoing(par, d, j):
@@ -155,9 +157,6 @@
                 if r < len(rounds):
                     tell_far(r)
 
-    for copy in loads[:2]:
-        copy.wait()
-
     def first_send(j, carry):
         send(0, j)
         return carry
@@ -165,8 +164,10 @@
     lax.fori_loop(0, chunks, first_send, 0)
 
     wave_copy.wait()
-    for copy in loads[2:12]:
+    for copy in loads[2:14]:
         copy.wait()
+    load(steps, lambda h: s_vec.at[:, :, h])
+    load(changes, lambda h: y_vec.at[:, :, h])
 
     def prepare(i, carry):
         at = pl.ds(pl.multiple_of(i * 8, 8), 8)
@@ -183,30 +184,26 @@
 
     lax.fori_loop(0, nx // 8, prepare, 0)
 
-    for copy in loads[12:]:
-        copy.wait()
-    wanted = [("sy", i, j) for i in range(PAIRS) for j in range(i, PAIRS)]
-    wanted += [("yy", i, j) for i in range(PAIRS) for j in range(i, PAIRS)]
-
-    def gram(i, sums):
-        at = pl.ds(pl.multiple_of(i * 8, 8), 8)
-        sums = list(sums)
-        for p in range(2):
-            for h in range(2):
-                s = [s_vec[k, p, h, at, :] for k in range(PAIRS)]
-                y = [y_vec[k, p, h, at, :] for k in range(PAIRS)]
-                for w, (kind, a, b) in enumerate(wanted):
-                    sums[w] = sums[w] + (s[a] if kind == "sy" else y[a]) * y[b]
-        return tuple(sums)
-
-    def total_of(x):
-        return jnp.sum(jnp.sum(x, axis=0, keepdims=True), axis=1, keepdims=True)
-
-    sums = lax.fori_loop(0, nx // 8, gram, (zero,) * len(wanted))
-    gram_row = jnp.zeros((1, LANES), jnp.float32)
-    for w, x in enumerate(sums):
-        gram_row = jnp.where(row_lane == 2 * PAIRS + w, total_of(x), gram_row)
-    row[...] = gram_row
+    for w in range(len(WANTED)):
+        products[w] = zero
+
+    def gram(j):
+        for w, (kind, a, b) in enumerate(WANTED):
+            part = products[w]
+            for i in range(ROWS // 8):
+                at = pl.ds(pl.multiple_of(j * ROWS + i * 8, 8), 8)
+                for p in range(2):
+                    for h in range(2):
+                        one = s_vec if kind == "sy" else y_vec
+                        part = part + one[a, p, h, at, :] * y_vec[b, p, h, at, :]
+            products[w] = part
+
+    def lanes_of(x, first):
+        n = x.shape[0]
+        sums = jnp.sum(jnp.sum(x, axis=1), axis=1, keepdims=True)
+        there = lax.broadcasted_iota(jnp.int32, (n, LANES), 1)
+        wanted = lax.broadcasted_iota(jnp.int32, (n, LANES), 0) + first
+        return jnp.sum(jnp.where(there == wanted, sums, 0.0), axis=0, keepdims=True)
 
     def along_y(v):
         back = [pltpu.roll(x, 1, 1) for x in v]
@@ -292,12 +289,22 @@
         wait_halo(cur, 0)
         acquaint(n)
 
+        @pl.when(n == 1)
+        def _():
+            for copy in loads[14:]:
+                copy.wait()
+
+        @pl.when(n == 2)
+        def _():
+            row[...] = lanes_of(products[...], 2 * PAIRS)
+
         def chunk(j, inside):
             pl.when(j + 1 < chunks)(lambda: wait_halo(cur, j + 1))
             pl.when(n >= 1)(lambda: wait_sent(nxt, j))
             for b in range(ROWS // 8):
                 block(cur, nxt, amplitude, pl.multiple_of(j * ROWS + b * 8, 8))
             send(nxt, j)
+            pl.when(n == 1)(lambda: gram(j))
             return inside
 
         return lax.fori_loop(0, chunks, chunk, carry)
@@ -320,28 +327,15 @@
 
     sums = lax.fori_loop(0, chunks, last_chunk, (zero,) * (2 * PAIRS))
 
-    mine = row[...]
-    for w, x in enumerate(sums):
-        mine = jnp.where(row_lane == w, total_of(x), mine)
-    row[...] = mine
-
-    spots = [(k,) for k in range(1, count)]
-    if count == 32:
-        spots = [(a, b, c) for a in range(4) for b in range(4) for c in range(2)][1:]
-        spots.sort(key=lambda t: -min(t[0], 4 - t[0]) - min(t[1], 4 - t[1]) - 0.1 * t[2])
-    core, along, slow = lax.rem(me, 2), lax.rem(me // 2, 4), me // 8
-    for k, spot in enumerate(spots):
-        if count == 32:
-            other = lax.rem(slow + spot[0], 4) * 8 + lax.rem(along + spot[1], 4) * 2
-            other = other + (1 - core if spot[2] else core)
-        else:
-            other = lax.rem(me + spot[0], count)
+    rows[pl.ds(me, 1)] = (row[...] + lanes_of(jnp.stack(sums), 0))[None]
+
+    for k in range(count - 1):
         pltpu.make_async_remote_copy(
-            src_ref=row,
-            dst_ref=rows.at[k],
+            src_ref=rows.at[me],
+            dst_ref=rows.at[me],
             send_sem=sum_send.at[0],
             recv_sem=sum_recv.at[0],
-            device_id={"gz": other},
+            device_id={"gz": k + jnp.where(me <= k, 1, 0)},
             device_id_type=MESH,
         ).start()
 
@@ -352,9 +346,10 @@
 
     lax.fori_loop(0, chunks, last_sent, 0)
 
+    others = rows.at[pl.ds(0, count - 1)]
     everyone = pltpu.make_async_remote_copy(
-        src_ref=rows,
-        dst_ref=rows,
+        src_ref=others,
+        dst_ref=others,
         send_sem=sum_send.at[0],
         recv_sem=sum_recv.at[0],
         device_id={"gz": lax.rem(me + 1, count)},
@@ -362,24 +357,46 @@
     )
     everyone.wait_send()
     everyone.wait_recv()
-    total = row[...] + jnp.sum(rows[...], axis=0)
+    total[...] = jnp.sum(rows[...], axis=0)
+
+
+def finish(
+    final, grad, s_vec, y_vec, total, out_field, out_gradient, out_direction, result, sem
+):
+    copies = []
+
+    def store(src, dst, h):
+        copy = pltpu.make_async_copy(
+            src, dst.at[..., pl.ds(h * LANES, LANES)], sem.at[len(copies)]
+        )
+        copy.start()
+        copies.append(copy)
+
+    for h in range(2):
+        store(final.at[:, :, h], out_field, h)
+        store(grad.at[:, h], out_gradient, h)
+
+    nx = grad.shape[2]
+    lane = lax.broadcasted_iota(jnp.int32, (1, LANES), 1)
+    sums = total[...]
 
     def value(k):
-        return jnp.sum(jnp.where(row_lane == k, total, 0.0), axis=1, keepdims=True)
+        return jnp.sum(jnp.where(lane == k, sums, 0.0), axis=1, keepdims=True)
 
     sg = [value(k) for k in range(PAIRS)]
     yg = [value(PAIRS + k) for k in range(PAIRS)]
     pair = {}
-    for w, (kind, a, b) in enumerate(wanted):
+    for w, (kind, a, b) in enumerate(WANTED):
         pair[kind, a, b] = value(2 * PAIRS + w)
         if kind == "yy":
             pair[kind, b, a] = pair[kind, a, b]
+    rho = [1.0 / pair["sy", i, i] for i in range(PAIRS)]
     alphas = [None] * PAIRS
     for i in reversed(range(PAIRS)):
         dot = sg[i]
-        for j in range(i + 1, PAIRS):
+        for j in reversed(range(i + 1, PAIRS)):
             dot = dot - alphas[j] * pair["sy", i, j]
-        alphas[i] = dot / pair["sy", i, i]
+        alphas[i] = dot * rho[i]
     gamma = pair["sy", PAIRS - 1, PAIRS - 1] / pair["yy", PAIRS - 1, PAIRS - 1]
     extra = []
     for i in range(PAIRS):
@@ -389,7 +406,7 @@
         dot = gamma * dot
         for j in range(i):
             dot = dot + extra[j] * pair["sy", j, i]
-        extra.append(alphas[i] - dot / pair["sy", i, i])
+        extra.append(alphas[i] - dot * rho[i])
 
     def wide(x):
         return jnp.broadcast_to(x, (8, LANES))
@@ -397,34 +414,22 @@
     of_g = wide(-gamma)
     of_y = [wide(gamma * alphas[i]) for i in range(PAIRS)]
     of_s = [wide(-extra[i]) for i in range(PAIRS)]
-
-    def combine(i, carry):
-        at = pl.ds(pl.multiple_of(i * 8, 8), 8)
-        for p in range(2):
+    for p in range(2):
+
+        def combine(i, carry):
+            at = pl.ds(pl.multiple_of(i * 8, 8), 8)
             for h in range(2):
-                out = of_g * grad[p, h, at, :]
+                parts = [of_g * grad[p, h, at, :], of_s[0] * s_vec[0, p, h, at, :]]
                 for k in range(PAIRS):
-                    out = out + of_y[k] * y_vec[k, p, h, at, :] + of_s[k] * s_vec[k, p, h, at, :]
-                spare[p, h, at, :] = out
-        return carry
-
-    lax.fori_loop(0, nx // 8, combine, 0)
-
-
-def write_out(final, grad, spare, out_field, out_gradient, out_direction, sem):
-    copies = []
-    for h in range(2):
-        half = pl.ds(h * LANES, LANES)
-        for src, dst in (
-            (final.at[:, :, h], out_field),
-            (grad.at[:, h], out_gradient),
-            (spare.at[:, h], out_direction),
-        ):
-            copies.append(
-                pltpu.make_async_copy(src, dst.at[..., half], sem.at[len(copies)])
-            )
-    for copy in copies:
-        copy.start()
+                    parts[0] = parts[0] + of_y[k] * y_vec[k, p, h, at, :]
+                    if k > 0:
+                        parts[1] = parts[1] + of_s[k] * s_vec[k, p, h, at, :]
+                result[p, h, at, :] = parts[0] + parts[1]
+            return carry
+
+        lax.fori_loop(0, nx // 8, combine, 0, unroll=4)
+        for h in range(2):
+            store(result.at[p, h], out_direction.at[p], h)
     for copy in copies:
         copy.wait()
 
@@ -446,10 +451,12 @@
         out_shape=(
             jax.ShapeDtypeStruct((3, *plane), f32),
             jax.ShapeDtypeStruct(plane, f32),
-            jax.ShapeDtypeStruct(plane, f32),
+            jax.ShapeDtypeStruct((PAIRS, *plane), f32),
+            jax.ShapeDtypeStruct((PAIRS, *plane), f32),
+            jax.ShapeDtypeStruct((1, LANES), f32),
         ),
         in_specs=in_specs,
-        out_specs=(vmem,) * 3,
+        out_specs=(vmem,) * 5,
         scratch_shapes=[
             pltpu.SMEM((STEPS,), f32),
             pltpu.VMEM((2, 3, 2, 2, padded, LANES), f32),
@@ -457,10 +464,10 @@
             pltpu.VMEM(plane, f32),
             pltpu.VMEM(plane, f32),
             pltpu.VMEM((3, *plane), f32),
-            pltpu.VMEM((PAIRS, *plane), f32),
-            pltpu.VMEM((PAIRS, *plane), f32),
+            pltpu.VMEM(plane, f32),
+            pltpu.VMEM((len(WANTED), 8, LANES), f32),
             pltpu.VMEM((1, LANES), f32),
-            pltpu.VMEM((count - 1, 1, LANES), f32),
+            pltpu.VMEM((count, 1, LANES), f32),
             pltpu.SemaphoreType.DMA((2, 2, chunks)),
             pltpu.SemaphoreType.DMA((2, 2, chunks)),
             pltpu.SemaphoreType.DMA((19,)),
@@ -474,17 +481,17 @@
         name="leapfrog",
     )(*[pltpu.with_memory_space_constraint(x, pltpu.HBM) for x in args])
     return pl.pallas_call(
-        write_out,
+        finish,
         out_shape=(
             jax.ShapeDtypeStruct(now.shape, f32),
             jax.ShapeDtypeStruct(lame.shape, f32),
             jax.ShapeDtypeStruct(lame.shape, f32),
         ),
-        in_specs=[vmem] * 3,
+        in_specs=[vmem] * 5,
         out_specs=(hbm,) * 3,
-        scratch_shapes=[pltpu.SemaphoreType.DMA((6,))],
+        scratch_shapes=[pltpu.VMEM(plane, f32), pltpu.SemaphoreType.DMA((8,))],
         compiler_params=pltpu.CompilerParams(vmem_limit_bytes=8 * 1024 * 1024),
-        name="write_out",
+        name="finish",
     )(*halves)
 
 

time: 59.5 us -> 59 us (level)
  Pallas kernels: 58.8 us -> 58.2 us
    pallas_call x1, Pallas kernels: 57.6 us -> 56.9 us  [on_device(): pl.pallas_call(kernel, out_shape=(jax.ShapeDtypeStruct((3, *plane), f32),...]
where the time goes in v2:
time: 59 us; the launch traced here: 58.8 us
  Pallas kernels  58.2 us (99%)
  between operations  0.64 us (1%)
    pallas_call x1, Pallas kernels, on_device(): pl.pallas_call(kernel, out_shape=(jax.ShapeDtypeStruct((3, *plane), f32),...  56.9 us
    pallas_call x1, Pallas kernels, on_device(): pl.pallas_call(finish, out_shape=(jax.ShapeDtypeStruct(now.shape, f32), j...  1.22 us

profile of v2, /device:TPU:1, one launch (start us, length us, event | category | flops | bytes accessed | tf_op | source)
XLA Modules:
  0.0 58.8 jit_solution(14649608002109568658)
XLA Ops:
  0.6 56.9 %leapfrog.1 = (f32[3,2,2,160,128]{4,3,2,1,0:T(8,128)S(1)}, f32[2,2,160,128]{3,2,1,0:T(8,128)S(1)}, f32[4,2,2,160,128]{4,3,2,1,0:T(8,128)S(1)}, f32[4,2,2,160,128]{4,3,2,1,0:T(8,128)S(1)}, f32[1,128]{1,0:T(1,128)S(1)}) custom-call(f32[3,2,160,256]{3,2,1,0:T(8,128)} %now.1, f32[3,2,160,256]{3,2,1,0:T(8,128)} %before.1, f32[2,160,256]{2,1,0:T(8,128)} %lame.1, ...), custom_call_target="tpu_custom_call" | custom-call | tf_op jit(solution)/shard_map/leapfrog/pallas_call | solution.py:449
  57.6 1.2 %finish.1 = (f32[3,2,160,256]{3,2,1,0:T(8,128)}, f32[2,160,256]{2,1,0:T(8,128)}, f32[2,160,256]{2,1,0:T(8,128)}) custom-call(f32[3,2,2,160,128]{4,3,2,1,0:T(8,128)S(1)} %get-tuple-element.8.final, f32[2,2,160,128]{3,2,1,0:T(8,128)S(1)} %get-tuple-element.9.grad, f32[4,2,2,160,128]{4,3,2,1,0:T(8,128)S(1)} %get-tuple-element.10.s_vec, ...), custom_call_target="tpu_custom_call" | custom-call | tf_op jit(solution)/shard_map/finish/pallas_call | solution.py:483

commit v3 on v2

--- a/solution.py
+++ b/solution.py
@@ -18,13 +18,14 @@
 def kernel(
     now, before, lame, shear, density, source, wave, prior, steps, changes,
     final, grad, s_vec, y_vec, total,
-    wavelet, field, halo, first_coef, second_coef, force, spare, products, row, rows,
-    send_sem, recv_sem, load_sem, hello_sem, sum_send, sum_recv,
+    wavelet, field, halo, bank, products, row, rows,
+    link_send, link_recv, pair_send, pair_recv, load_sem, hello_sem, sum_send, sum_recv,
 ):
     me = lax.axis_index("gz")
     count = lax.axis_size("gz")
-    nx = first_coef.shape[2]
+    nx = grad.shape[2]
     chunks = nx // ROWS
+    half = chunks // 2
     padded = nx + 2 * PAD
     zero = jnp.zeros((8, LANES), jnp.float32)
     lane = lax.broadcasted_iota(jnp.int32, (8, LANES), 1)
@@ -32,27 +33,34 @@
     at_start = lane == 0
     at_end = lane == LANES - 1
     exists = (me > 0, me < count - 1)
-    beside = (jnp.maximum(me - 1, 0), jnp.minimum(me + 1, count - 1))
+    first_coef, second_coef, density_of, prior_of = (bank.at[k] for k in range(4))
+    force = bank.at[pl.ds(4, 3)]
+
+    core = lax.rem(me, 2)
+    pair, link = 1 - core, core
+    pair_peer = me + 1 - 2 * core
+    linked = jnp.logical_and(me + 2 * core - 1 >= 0, me + 2 * core - 1 < count)
+    link_peer = jnp.clip(me + 2 * core - 1, 0, count - 1)
+
+    barrier = pltpu.get_barrier_semaphore()
+    pl.semaphore_signal(barrier, inc=1, device_id={"gz": pair_peer}, device_id_type=MESH)
+
+    @pl.when(linked)
+    def _():
+        pl.semaphore_signal(barrier, inc=1, device_id={"gz": link_peer}, device_id_type=MESH)
 
     inner = pl.ds(PAD, nx)
-    loads = []
-
-    def load(src, dst_of):
+
+    def load(src, dst_of, group):
         for h in range(2):
-            copy = pltpu.make_async_copy(
-                src.at[..., pl.ds(h * LANES, LANES)], dst_of(h), load_sem.at[len(loads)]
-            )
-            copy.start()
-            loads.append(copy)
-
-    barrier = pltpu.get_barrier_semaphore()
-    for d in range(2):
-
-        @pl.when(exists[d])
-        def _():
-            pl.semaphore_signal(barrier, inc=1, device_id={"gz": beside[d]}, device_id_type=MESH)
-
-    load(now, lambda h: field.at[0, :, :, h, inner, :])
+            pltpu.make_async_copy(
+                src.at[..., pl.ds(h * LANES, LANES)], dst_of(h), load_sem.at[group]
+            ).start()
+
+    def loaded(dst, group):
+        pltpu.make_async_copy(dst, dst, load_sem.at[group]).wait()
+
+    load(now, lambda h: field.at[0, :, :, h, inner, :], 0)
 
     for par in range(2):
         for c in range(3):
@@ -75,51 +83,106 @@
 
             lax.fori_loop(0, padded // 8, clear, 0)
 
-    for copy in loads:
-        copy.wait()
-    wave_copy = pltpu.make_async_copy(wave, wavelet, load_sem.at[18])
-    wave_copy.start()
-    load(lame, lambda h: first_coef.at[:, h])
-    load(shear, lambda h: second_coef.at[:, h])
-    load(density, lambda h: spare.at[:, h])
-    load(source, lambda h: force.at[:, :, h])
-    load(prior, lambda h: grad.at[:, h])
-    load(before, lambda h: field.at[1, :, :, h, inner, :])
-    pl.semaphore_wait(barrier, jnp.where(me > 0, 1, 0) + jnp.where(me < count - 1, 1, 0))
-
-    def outgoing(par, d, j):
-        at = pl.ds(pl.multiple_of(PAD + j * ROWS, 8), ROWS)
+    pl.semaphore_wait(barrier, jnp.where(linked, 2, 1))
+
+    def link_rows(j):
+        return pl.multiple_of(j * ROWS, 8), ROWS
+
+    def pair_rows(i):
+        return i * half * ROWS, half * ROWS
+
+    def over_link(par, start, size, sem):
+        at = pl.ds(PAD + start, size)
         return pltpu.make_async_remote_copy(
-            src_ref=field.at[par, :, d, :, at, :],
-            dst_ref=halo.at[par, 1 - d, :, :, at, :],
-            send_sem=send_sem.at[par, d, j],
-            recv_sem=recv_sem.at[par, 1 - d, j],
-            device_id={"gz": beside[d]},
+            src_ref=field.at[par, :, link, :, at, :],
+            dst_ref=halo.at[par, 1 - link, :, :, at, :],
+            send_sem=link_send.at[par],
+            recv_sem=link_recv.at[par, sem],
+            device_id={"gz": link_peer},
             device_id_type=MESH,
         )
 
-    def incoming(par, d, j):
-        at = pl.ds(pl.multiple_of(PAD + j * ROWS, 8), ROWS)
+    def to_pair(par, start, size, sem):
+        at = pl.ds(PAD + start, size)
         return pltpu.make_async_remote_copy(
-            src_ref=field.at[par, :, d, :, at, :],
-            dst_ref=halo.at[par, d, :, :, at, :],
-            send_sem=send_sem.at[par, d, j],
-            recv_sem=recv_sem.at[par, d, j],
-            device_id={"gz": beside[d]},
+            src_ref=field.at[par, :, pair, :, at, :],
+            dst_ref=halo.at[par, 1 - pair, :, :, at, :],
+            send_sem=pair_send.at[par],
+            recv_sem=pair_recv.at[par, sem],
+            device_id={"gz": pair_peer},
             device_id_type=MESH,
         )
 
-    def send(par, j):
-        for d in range(2):
-            pl.when(exists[d])(lambda d=d: outgoing(par, d, j).start())
-
-    def wait_sent(par, j):
-        for d in range(2):
-            pl.when(exists[d])(lambda d=d: outgoing(par, d, j).wait_send())
-
-    def wait_halo(par, j):
-        for d in range(2):
-            pl.when(exists[d])(lambda d=d: incoming(par, d, j).wait_recv())
+    def from_argument(direction, start, size, h, send_sem, recv_sem, peer):
+        pltpu.make_async_remote_copy(
+            src_ref=now.at[:, direction, pl.ds(start, size), pl.ds(h * LANES, LANES)],
+            dst_ref=halo.at[0, 1 - direction, :, h, pl.ds(PAD + start, size), :],
+            send_sem=send_sem,
+            recv_sem=recv_sem,
+            device_id={"gz": peer},
+            device_id_type=MESH,
+        ).start()
+
+    def first_send(j, carry):
+        for h in range(2):
+            from_argument(
+                link, *link_rows(j), h, link_send.at[0], link_recv.at[0, j], link_peer
+            )
+        return carry
+
+    @pl.when(linked)
+    def _():
+        lax.fori_loop(0, chunks, first_send, 0)
+
+    for i in range(2):
+        for h in range(2):
+            from_argument(
+                pair, *pair_rows(i), h, pair_send.at[0], pair_recv.at[0, i], pair_peer
+            )
+    wave_copy = pltpu.make_async_copy(wave, wavelet, load_sem.at[3])
+    wave_copy.start()
+    load(lame, lambda h: first_coef.at[:, h], 1)
+    load(shear, lambda h: second_coef.at[:, h], 1)
+    load(density, lambda h: density_of.at[:, h], 1)
+    load(prior, lambda h: prior_of.at[:, h], 1)
+    load(source, lambda h: force.at[:, :, h], 1)
+    load(before, lambda h: field.at[1, :, :, h, inner, :], 2)
+
+    def send_link(par, j):
+        pl.when(linked)(lambda: over_link(par, *link_rows(j), j).start())
+
+    def send_pair(par, i):
+        to_pair(par, *pair_rows(i), i).start()
+
+    def wait_sent(par):
+        to_pair(par, 0, nx, 0).wait_send()
+        pl.when(linked)(lambda: over_link(par, 0, nx, 0).wait_send())
+
+    def wait_link(par, j):
+        @pl.when(linked)
+        def _():
+            start, size = link_rows(j)
+            at = pl.ds(PAD + start, size)
+            pltpu.make_async_remote_copy(
+                src_ref=field.at[par, :, link, :, at, :],
+                dst_ref=halo.at[par, link, :, :, at, :],
+                send_sem=link_send.at[par],
+                recv_sem=link_recv.at[par, j],
+                device_id={"gz": link_peer},
+                device_id_type=MESH,
+            ).wait_recv()
+
+    def wait_pair(par, i):
+        start, size = pair_rows(i)
+        at = pl.ds(PAD + start, size)
+        pltpu.make_async_remote_copy(
+            src_ref=field.at[par, :, pair, :, at, :],
+            dst_ref=halo.at[par, pair, :, :, at, :],
+            send_sem=pair_send.at[par],
+            recv_sem=pair_recv.at[par, i],
+            device_id={"gz": pair_peer},
+            device_id_type=MESH,
+        ).wait_recv()
 
     rounds = []
     while 4 << len(rounds) < count:
@@ -137,15 +200,12 @@
             @pl.when(within(r, d))
             def _():
                 pl.semaphore_signal(
-                    hello_sem.at[r, 1 - d], inc=1, device_id={"gz": far(r, d)}, device_id_type=MESH
+                    hello_sem.at[r], inc=1, device_id={"gz": far(r, d)}, device_id_type=MESH
                 )
 
     def hear_far(r):
-        for d in range(2):
-
-            @pl.when(within(r, d))
-            def _():
-                pl.semaphore_wait(hello_sem.at[r, d], 1)
+        heard = jnp.where(within(r, 0), 1, 0) + jnp.where(within(r, 1), 1, 0)
+        pl.when(heard > 0)(lambda: pl.semaphore_wait(hello_sem.at[r], heard))
 
     def acquaint(n):
         for r in range(len(rounds) + 1):
@@ -157,27 +217,23 @@
                 if r < len(rounds):
                     tell_far(r)
 
-    def first_send(j, carry):
-        send(0, j)
-        return carry
-
-    lax.fori_loop(0, chunks, first_send, 0)
 
     wave_copy.wait()
-    for copy in loads[2:14]:
-        copy.wait()
-    load(steps, lambda h: s_vec.at[:, :, h])
-    load(changes, lambda h: y_vec.at[:, :, h])
+    loaded(bank, 1)
+    loaded(field.at[0, :, :, :, inner, :], 0)
+    loaded(field.at[1, :, :, :, inner, :], 2)
+    load(steps, lambda h: s_vec.at[:, :, h], 4)
+    load(changes, lambda h: y_vec.at[:, :, h], 5)
 
     def prepare(i, carry):
         at = pl.ds(pl.multiple_of(i * 8, 8), 8)
         for p in range(2):
             for h in range(2):
                 mu = second_coef[p, h, at, :]
-                coeff = 0.04 / spare[p, h, at, :]
+                coeff = 0.04 / density_of[p, h, at, :]
                 first_coef[p, h, at, :] = 0.25 * coeff * (first_coef[p, h, at, :] + mu)
                 second_coef[p, h, at, :] = coeff * mu
-                grad[p, h, at, :] = mu - grad[p, h, at, :]
+                grad[p, h, at, :] = mu - prior_of[p, h, at, :]
                 for c in range(3):
                     force[c, p, h, at, :] = coeff * force[c, p, h, at, :]
         return carry
@@ -286,36 +342,43 @@
         cur = lax.rem(n, 2)
         nxt = 1 - cur
         amplitude = wavelet[n]
-        wait_halo(cur, 0)
+        wait_link(cur, 0)
+        wait_pair(cur, 0)
+        pl.when(n >= 1)(lambda: wait_sent(nxt))
         acquaint(n)
 
         @pl.when(n == 1)
         def _():
-            for copy in loads[14:]:
-                copy.wait()
+            loaded(s_vec, 4)
+            loaded(y_vec, 5)
 
         @pl.when(n == 2)
         def _():
             row[...] = lanes_of(products[...], 2 * PAIRS)
 
         def chunk(j, inside):
-            pl.when(j + 1 < chunks)(lambda: wait_halo(cur, j + 1))
-            pl.when(n >= 1)(lambda: wait_sent(nxt, j))
+            pl.when(j + 1 < chunks)(lambda: wait_link(cur, j + 1))
+            pl.when(j == half - 1)(lambda: wait_pair(cur, 1))
             for b in range(ROWS // 8):
                 block(cur, nxt, amplitude, pl.multiple_of(j * ROWS + b * 8, 8))
-            send(nxt, j)
+            send_link(nxt, j)
+            pl.when(j == half - 1)(lambda: send_pair(nxt, 0))
             pl.when(n == 1)(lambda: gram(j))
             return inside
 
-        return lax.fori_loop(0, chunks, chunk, carry)
+        lax.fori_loop(0, chunks, chunk, 0)
+        send_pair(nxt, 1)
+        return carry
 
     lax.fori_loop(0, STEPS - 1, step, 0)
 
     cur, nxt = (STEPS - 1) % 2, STEPS % 2
-    wait_halo(cur, 0)
+    wait_link(cur, 0)
+    wait_pair(cur, 0)
 
     def last_chunk(j, sums):
-        pl.when(j + 1 < chunks)(lambda: wait_halo(cur, j + 1))
+        pl.when(j + 1 < chunks)(lambda: wait_link(cur, j + 1))
+        pl.when(j == half - 1)(lambda: wait_pair(cur, 1))
         sums = list(sums)
         for b in range(ROWS // 8):
             base = pl.multiple_of(j * ROWS + b * 8, 8)
@@ -339,12 +402,8 @@
             device_id_type=MESH,
         ).start()
 
-    def last_sent(j, carry):
-        wait_sent(nxt, j)
-        wait_sent(cur, j)
-        return carry
-
-    lax.fori_loop(0, chunks, last_sent, 0)
+    wait_sent(nxt)
+    wait_sent(cur)
 
     others = rows.at[pl.ds(0, count - 1)]
     everyone = pltpu.make_async_remote_copy(
@@ -363,18 +422,12 @@
 def finish(
     final, grad, s_vec, y_vec, total, out_field, out_gradient, out_direction, result, sem
 ):
-    copies = []
-
-    def store(src, dst, h):
-        copy = pltpu.make_async_copy(
-            src, dst.at[..., pl.ds(h * LANES, LANES)], sem.at[len(copies)]
-        )
-        copy.start()
-        copies.append(copy)
+    def store(src, dst, h, group):
+        pltpu.make_async_copy(src, dst.at[..., pl.ds(h * LANES, LANES)], sem.at[group]).start()
 
     for h in range(2):
-        store(final.at[:, :, h], out_field, h)
-        store(grad.at[:, h], out_gradient, h)
+        store(final.at[:, :, h], out_field, h, 0)
+        store(grad.at[:, h], out_gradient, h, 1)
 
     nx = grad.shape[2]
     lane = lax.broadcasted_iota(jnp.int32, (1, LANES), 1)
@@ -429,9 +482,9 @@
 
         lax.fori_loop(0, nx // 8, combine, 0, unroll=4)
         for h in range(2):
-            store(result.at[p, h], out_direction.at[p], h)
-    for copy in copies:
-        copy.wait()
+            store(result.at[p, h], out_direction.at[p], h, 2)
+    for group, out in enumerate((out_field, out_gradient, out_direction)):
+        pltpu.make_async_copy(out, out, sem.at[group]).wait()
 
 
 def on_device(*args):
@@ -461,17 +514,16 @@
             pltpu.SMEM((STEPS,), f32),
             pltpu.VMEM((2, 3, 2, 2, padded, LANES), f32),
             pltpu.VMEM((2, 2, 3, 2, padded, LANES), f32),
-            pltpu.VMEM(plane, f32),
-            pltpu.VMEM(plane, f32),
-            pltpu.VMEM((3, *plane), f32),
-            pltpu.VMEM(plane, f32),
+            pltpu.VMEM((7, *plane), f32),
             pltpu.VMEM((len(WANTED), 8, LANES), f32),
             pltpu.VMEM((1, LANES), f32),
             pltpu.VMEM((count, 1, LANES), f32),
-            pltpu.SemaphoreType.DMA((2, 2, chunks)),
-            pltpu.SemaphoreType.DMA((2, 2, chunks)),
-            pltpu.SemaphoreType.DMA((19,)),
-            pltpu.SemaphoreType.REGULAR((3, 2)),
+            pltpu.SemaphoreType.DMA((2,)),
+            pltpu.SemaphoreType.DMA((2, chunks)),
+            pltpu.SemaphoreType.DMA((2,)),
+            pltpu.SemaphoreType.DMA((2, 2)),
+            pltpu.SemaphoreType.DMA((6,)),
+            pltpu.SemaphoreType.REGULAR((3,)),
             pltpu.SemaphoreType.DMA((1,)),
             pltpu.SemaphoreType.DMA((1,)),
         ],
@@ -489,7 +541,7 @@
         ),
         in_specs=[vmem] * 5,
         out_specs=(hbm,) * 3,
-        scratch_shapes=[pltpu.VMEM(plane, f32), pltpu.SemaphoreType.DMA((8,))],
+        scratch_shapes=[pltpu.VMEM(plane, f32), pltpu.SemaphoreType.DMA((3,))],
         compiler_params=pltpu.CompilerParams(vmem_limit_bytes=8 * 1024 * 1024),
         name="finish",
     )(*halves)

time: 59 us -> 58.5 us (level)
  no operation moved by 1% of the time
where the time goes in v3:
time: 58.5 us; the launch traced here: 58.4 us
  Pallas kernels  57.7 us (99%)
  between operations  0.64 us (1%)
    pallas_call x1, Pallas kernels, on_device(): pl.pallas_call(kernel, out_shape=(jax.ShapeDtypeStruct((3, *plane), f32),...  56.5 us
    pallas_call x1, Pallas kernels, on_device(): pl.pallas_call(finish, out_shape=(jax.ShapeDtypeStruct(now.shape, f32), j...  1.18 us

profile of v3, /device:TPU:1, one launch (start us, length us, event | category | flops | bytes accessed | tf_op | source)
XLA Modules:
  0.0 58.4 jit_solution(3849320985763475516)
XLA Ops:
  0.6 56.5 %leapfrog.1 = (f32[3,2,2,160,128]{4,3,2,1,0:T(8,128)S(1)}, f32[2,2,160,128]{3,2,1,0:T(8,128)S(1)}, f32[4,2,2,160,128]{4,3,2,1,0:T(8,128)S(1)}, f32[4,2,2,160,128]{4,3,2,1,0:T(8,128)S(1)}, f32[1,128]{1,0:T(1,128)S(1)}) custom-call(f32[3,2,160,256]{3,2,1,0:T(8,128)} %now.1, f32[3,2,160,256]{3,2,1,0:T(8,128)} %before.1, f32[2,160,256]{2,1,0:T(8,128)} %lame.1, ...), custom_call_target="tpu_custom_call" | custom-call | tf_op jit(solution)/shard_map/leapfrog/pallas_call | solution.py:502
  57.2 1.2 %finish.1 = (f32[3,2,160,256]{3,2,1,0:T(8,128)}, f32[2,160,256]{2,1,0:T(8,128)}, f32[2,160,256]{2,1,0:T(8,128)}) custom-call(f32[3,2,2,160,128]{4,3,2,1,0:T(8,128)S(1)} %get-tuple-element.8.final, f32[2,2,160,128]{3,2,1,0:T(8,128)S(1)} %get-tuple-element.9.grad, f32[4,2,2,160,128]{4,3,2,1,0:T(8,128)S(1)} %get-tuple-element.10.s_vec, ...), custom_call_target="tpu_custom_call" | custom-call | tf_op jit(solution)/shard_map/finish/pallas_call | solution.py:535

commit v4 on v3

--- a/solution.py
+++ b/solution.py
@@ -9,7 +9,8 @@
 PAIRS = 4
 WANTED = [("sy", i, j) for i in range(PAIRS) for j in range(i, PAIRS)]
 WANTED += [("yy", i, j) for i in range(PAIRS) for j in range(i, PAIRS)]
-ROWS = 16
+ROWS = 24
+REST = 16
 PAD = 8
 LANES = 128
 MESH = pl.DeviceIdType.MESH
@@ -24,8 +25,8 @@
     me = lax.axis_index("gz")
     count = lax.axis_size("gz")
     nx = grad.shape[2]
-    chunks = nx // ROWS
-    half = chunks // 2
+    last = (nx - REST) // ROWS
+    split = (last + 1) // 2
     padded = nx + 2 * PAD
     zero = jnp.zeros((8, LANES), jnp.float32)
     lane = lax.broadcasted_iota(jnp.int32, (8, LANES), 1)
@@ -86,10 +87,12 @@
     pl.semaphore_wait(barrier, jnp.where(linked, 2, 1))
 
     def link_rows(j):
+        if isinstance(j, int):
+            return j * ROWS, REST if j == last else ROWS
         return pl.multiple_of(j * ROWS, 8), ROWS
 
     def pair_rows(i):
-        return i * half * ROWS, half * ROWS
+        return (split * ROWS, nx - split * ROWS) if i else (0, split * ROWS)
 
     def over_link(par, start, size, sem):
         at = pl.ds(PAD + start, size)
@@ -132,7 +135,8 @@
 
     @pl.when(linked)
     def _():
-        lax.fori_loop(0, chunks, first_send, 0)
+        lax.fori_loop(0, last, first_send, 0)
+        first_send(last, 0)
 
     for i in range(2):
         for h in range(2):
@@ -210,7 +214,7 @@
     def acquaint(n):
         for r in range(len(rounds) + 1):
 
-            @pl.when(n == 2 + r)
+            @pl.when(n == 3 + r)
             def _():
                 if r > 0:
                     hear_far(r - 1)
@@ -243,11 +247,11 @@
     for w in range(len(WANTED)):
         products[w] = zero
 
-    def gram(j):
+    def gram(bases):
         for w, (kind, a, b) in enumerate(WANTED):
             part = products[w]
-            for i in range(ROWS // 8):
-                at = pl.ds(pl.multiple_of(j * ROWS + i * 8, 8), 8)
+            for base in bases:
+                at = pl.ds(base, 8)
                 for p in range(2):
                     for h in range(2):
                         one = s_vec if kind == "sy" else y_vec
@@ -338,12 +342,40 @@
                 grads.append((z, h, new))
         return grads
 
+    def sweep(cur, nxt, amplitude, out, after, ending, carry):
+        def at_split(j, act):
+            if isinstance(j, int):
+                if j == split:
+                    act()
+            else:
+                pl.when(j == split)(act)
+
+        def part(j, bases, carry):
+            wait_link(cur, j)
+            at_split(j, lambda: wait_pair(cur, 1))
+            for i, base in enumerate(bases):
+                carry = after(base, block(cur, nxt, amplitude, base, out), carry)
+                if i == 0 and out is None and not (isinstance(j, int) and j == 0):
+                    send_link(nxt, j - 1)
+                    at_split(j, lambda: send_pair(nxt, 0))
+            ending(bases)
+            return carry
+
+        def later(j, carry):
+            return part(j, [pl.multiple_of(j * ROWS + k, 8) for k in (-8, 0, 8)], carry)
+
+        wait_pair(cur, 0)
+        carry = part(0, [0, 8], carry)
+        carry = lax.fori_loop(1, last, later, carry)
+        carry = part(last, [last * ROWS + k for k in (-8, 0, 8)], carry)
+        if out is None:
+            send_link(nxt, last)
+            send_pair(nxt, 1)
+        return carry
+
     def step(n, carry):
         cur = lax.rem(n, 2)
         nxt = 1 - cur
-        amplitude = wavelet[n]
-        wait_link(cur, 0)
-        wait_pair(cur, 0)
         pl.when(n >= 1)(lambda: wait_sent(nxt))
         acquaint(n)
 
@@ -356,39 +388,37 @@
         def _():
             row[...] = lanes_of(products[...], 2 * PAIRS)
 
-        def chunk(j, inside):
-            pl.when(j + 1 < chunks)(lambda: wait_link(cur, j + 1))
-            pl.when(j == half - 1)(lambda: wait_pair(cur, 1))
-            for b in range(ROWS // 8):
-                block(cur, nxt, amplitude, pl.multiple_of(j * ROWS + b * 8, 8))
-            send_link(nxt, j)
-            pl.when(j == half - 1)(lambda: send_pair(nxt, 0))
-            pl.when(n == 1)(lambda: gram(j))
-            return inside
-
-        lax.fori_loop(0, chunks, chunk, 0)
-        send_pair(nxt, 1)
-        return carry
+        return sweep(
+            cur,
+            nxt,
+            wavelet[n],
+            None,
+            lambda base, grads, carry: carry,
+            lambda bases: pl.when(n == 1)(lambda: gram(bases)),
+            carry,
+        )
 
     lax.fori_loop(0, STEPS - 1, step, 0)
 
     cur, nxt = (STEPS - 1) % 2, STEPS % 2
-    wait_link(cur, 0)
-    wait_pair(cur, 0)
-
-    def last_chunk(j, sums):
-        pl.when(j + 1 < chunks)(lambda: wait_link(cur, j + 1))
-        pl.when(j == half - 1)(lambda: wait_pair(cur, 1))
+
+    def multiply(base, grads, sums):
         sums = list(sums)
-        for b in range(ROWS // 8):
-            base = pl.multiple_of(j * ROWS + b * 8, 8)
-            for z, h, g in block(cur, nxt, wavelet[STEPS - 1], base, final):
-                for k in range(PAIRS):
-                    sums[k] = sums[k] + s_vec[k, z, h, pl.ds(base, 8), :] * g
-                    sums[PAIRS + k] = sums[PAIRS + k] + y_vec[k, z, h, pl.ds(base, 8), :] * g
+        for z, h, g in grads:
+            for k in range(PAIRS):
+                sums[k] = sums[k] + s_vec[k, z, h, pl.ds(base, 8), :] * g
+                sums[PAIRS + k] = sums[PAIRS + k] + y_vec[k, z, h, pl.ds(base, 8), :] * g
         return tuple(sums)
 
-    sums = lax.fori_loop(0, chunks, last_chunk, (zero,) * (2 * PAIRS))
+    sums = sweep(
+        cur,
+        nxt,
+        wavelet[STEPS - 1],
+        final,
+        multiply,
+        lambda bases: None,
+        (zero,) * (2 * PAIRS),
+    )
 
     rows[pl.ds(me, 1)] = (row[...] + lanes_of(jnp.stack(sums), 0))[None]
 
@@ -493,7 +523,7 @@
     nx = now.shape[2]
     count = lax.axis_size("gz")
     padded = nx + 2 * PAD
-    chunks = nx // ROWS
+    chunks = (nx - REST) // ROWS + 1
     f32 = jnp.float32
     hbm = pl.BlockSpec(memory_space=pltpu.HBM)
     vmem = pl.BlockSpec(memory_space=pltpu.VMEM)

time: 58.5 us -> 58.3 us (level)
  no operation moved by 1% of the time
where the time goes in v4:
time: 58.3 us; the launch traced here: 58.1 us
  Pallas kernels  57.5 us (99%)
  between operations  0.64 us (1%)
    pallas_call x1, Pallas kernels, on_device(): pl.pallas_call(kernel, out_shape=(jax.ShapeDtypeStruct((3, *plane), f32),...  56.3 us
    pallas_call x1, Pallas kernels, on_device(): pl.pallas_call(finish, out_shape=(jax.ShapeDtypeStruct(now.shape, f32), j...  1.18 us

profile of v4, /device:TPU:1, one launch (start us, length us, event | category | flops | bytes accessed | tf_op | source)
XLA Modules:
  0.0 58.1 jit_solution(8965515314818003241)
XLA Ops:
  0.6 56.3 %leapfrog.1 = (f32[3,2,2,160,128]{4,3,2,1,0:T(8,128)S(1)}, f32[2,2,160,128]{3,2,1,0:T(8,128)S(1)}, f32[4,2,2,160,128]{4,3,2,1,0:T(8,128)S(1)}, f32[4,2,2,160,128]{4,3,2,1,0:T(8,128)S(1)}, f32[1,128]{1,0:T(1,128)S(1)}) custom-call(f32[3,2,160,256]{3,2,1,0:T(8,128)} %now.1, f32[3,2,160,256]{3,2,1,0:T(8,128)} %before.1, f32[2,160,256]{2,1,0:T(8,128)} %lame.1, ...), custom_call_target="tpu_custom_call" | custom-call | tf_op jit(solution)/shard_map/leapfrog/pallas_call | solution.py:532
  57.0 1.2 %finish.1 = (f32[3,2,160,256]{3,2,1,0:T(8,128)}, f32[2,160,256]{2,1,0:T(8,128)}, f32[2,160,256]{2,1,0:T(8,128)}) custom-call(f32[3,2,2,160,128]{4,3,2,1,0:T(8,128)S(1)} %get-tuple-element.8.final, f32[2,2,160,128]{3,2,1,0:T(8,128)S(1)} %get-tuple-element.9.grad, f32[4,2,2,160,128]{4,3,2,1,0:T(8,128)S(1)} %get-tuple-element.10.s_vec, ...), custom_call_target="tpu_custom_call" | custom-call | tf_op jit(solution)/shard_map/finish/pallas_call | solution.py:565

commit v5 on v4

--- a/solution.py
+++ b/solution.py
@@ -9,7 +9,7 @@
 PAIRS = 4
 WANTED = [("sy", i, j) for i in range(PAIRS) for j in range(i, PAIRS)]
 WANTED += [("yy", i, j) for i in range(PAIRS) for j in range(i, PAIRS)]
-ROWS = 24
+ROWS = 16
 REST = 16
 PAD = 8
 LANES = 128
@@ -133,10 +133,23 @@
             )
         return carry
 
-    @pl.when(linked)
+    around = jnp.logical_and(linked, lax.rem(me + core, 8) == 0)
+
+    @pl.when(jnp.logical_and(linked, jnp.logical_not(around)))
     def _():
         lax.fori_loop(0, last, first_send, 0)
         first_send(last, 0)
+
+    @pl.when(around)
+    def _():
+        loaded(field.at[0, :, :, :, inner, :], 0)
+
+        def loaded_send(j, carry):
+            over_link(0, *link_rows(j), j).start()
+            return carry
+
+        lax.fori_loop(0, last, loaded_send, 0)
+        over_link(0, *link_rows(last), last).start()
 
     for i in range(2):
         for h in range(2):
@@ -224,7 +237,7 @@
 
     wave_copy.wait()
     loaded(bank, 1)
-    loaded(field.at[0, :, :, :, inner, :], 0)
+    pl.when(jnp.logical_not(around))(lambda: loaded(field.at[0, :, :, :, inner, :], 0))
     loaded(field.at[1, :, :, :, inner, :], 2)
     load(steps, lambda h: s_vec.at[:, :, h], 4)
     load(changes, lambda h: y_vec.at[:, :, h], 5)
@@ -362,12 +375,12 @@
             return carry
 
         def later(j, carry):
-            return part(j, [pl.multiple_of(j * ROWS + k, 8) for k in (-8, 0, 8)], carry)
+            return part(j, [pl.multiple_of(j * ROWS + k, 8) for k in range(-8, ROWS - 8, 8)], carry)
 
         wait_pair(cur, 0)
-        carry = part(0, [0, 8], carry)
+        carry = part(0, list(range(0, ROWS - 8, 8)), carry)
         carry = lax.fori_loop(1, last, later, carry)
-        carry = part(last, [last * ROWS + k for k in (-8, 0, 8)], carry)
+        carry = part(last, [last * ROWS + k for k in range(-8, REST, 8)], carry)
         if out is None:
             send_link(nxt, last)
             send_pair(nxt, 1)

time: 58.3 us -> 58.1 us (level)
  no operation moved by 1% of the time
where the time goes in v5:
time: 58.1 us; the launch traced here: 58 us
  Pallas kernels  57.3 us (99%)
  between operations  0.64 us (1%)
    pallas_call x1, Pallas kernels, on_device(): pl.pallas_call(kernel, out_shape=(jax.ShapeDtypeStruct((3, *plane), f32),...  56.2 us
    pallas_call x1, Pallas kernels, on_device(): pl.pallas_call(finish, out_shape=(jax.ShapeDtypeStruct(now.shape, f32), j...  1.18 us

profile of v5, /device:TPU:1, one launch (start us, length us, event | category | flops | bytes accessed | tf_op | source)
XLA Modules:
  0.0 58.0 jit_solution(8467310349384735258)
XLA Ops:
  0.6 56.2 %leapfrog.1 = (f32[3,2,2,160,128]{4,3,2,1,0:T(8,128)S(1)}, f32[2,2,160,128]{3,2,1,0:T(8,128)S(1)}, f32[4,2,2,160,128]{4,3,2,1,0:T(8,128)S(1)}, f32[4,2,2,160,128]{4,3,2,1,0:T(8,128)S(1)}, f32[1,128]{1,0:T(1,128)S(1)}) custom-call(f32[3,2,160,256]{3,2,1,0:T(8,128)} %now.1, f32[3,2,160,256]{3,2,1,0:T(8,128)} %before.1, f32[2,160,256]{2,1,0:T(8,128)} %lame.1, ...), custom_call_target="tpu_custom_call" | custom-call | tf_op jit(solution)/shard_map/leapfrog/pallas_call | solution.py:545
  56.8 1.2 %finish.1 = (f32[3,2,160,256]{3,2,1,0:T(8,128)}, f32[2,160,256]{2,1,0:T(8,128)}, f32[2,160,256]{2,1,0:T(8,128)}) custom-call(f32[3,2,2,160,128]{4,3,2,1,0:T(8,128)S(1)} %get-tuple-element.8.final, f32[2,2,160,128]{3,2,1,0:T(8,128)S(1)} %get-tuple-element.9.grad, f32[4,2,2,160,128]{4,3,2,1,0:T(8,128)S(1)} %get-tuple-element.10.s_vec, ...), custom_call_target="tpu_custom_call" | custom-call | tf_op jit(solution)/shard_map/finish/pallas_call | solution.py:578

commit v6 on v5

--- a/solution.py
+++ b/solution.py
@@ -386,8 +386,7 @@
             send_pair(nxt, 1)
         return carry
 
-    def step(n, carry):
-        cur = lax.rem(n, 2)
+    def step(n, cur, carry):
         nxt = 1 - cur
         pl.when(n >= 1)(lambda: wait_sent(nxt))
         acquaint(n)
@@ -411,7 +410,11 @@
             carry,
         )
 
-    lax.fori_loop(0, STEPS - 1, step, 0)
+    def two_steps(k, carry):
+        return step(2 * k + 1, 1, step(2 * k, 0, carry))
+
+    lax.fori_loop(0, STEPS // 2 - 1, two_steps, 0)
+    lax.fori_loop(STEPS // 2 - 1, STEPS // 2, lambda k, carry: step(2 * k, 0, carry), 0)
 
     cur, nxt = (STEPS - 1) % 2, STEPS % 2
 

time: 58.1 us -> 58.1 us (level)
  no operation moved by 1% of the time
where the time goes in v6:
time: 58.1 us; the launch traced here: 58 us
  Pallas kernels  57.3 us (99%)
  between operations  0.64 us (1%)
    pallas_call x1, Pallas kernels, on_device(): pl.pallas_call(kernel, out_shape=(jax.ShapeDtypeStruct((3, *plane), f32),...  56.2 us
    pallas_call x1, Pallas kernels, on_device(): pl.pallas_call(finish, out_shape=(jax.ShapeDtypeStruct(now.shape, f32), j...  1.18 us

profile of v6, /device:TPU:1, one launch (start us, length us, event | category | flops | bytes accessed | tf_op | source)
XLA Modules:
  0.0 58.0 jit_solution(7479542929083456756)
XLA Ops:
  0.6 56.2 %leapfrog.1 = (f32[3,2,2,160,128]{4,3,2,1,0:T(8,128)S(1)}, f32[2,2,160,128]{3,2,1,0:T(8,128)S(1)}, f32[4,2,2,160,128]{4,3,2,1,0:T(8,128)S(1)}, f32[4,2,2,160,128]{4,3,2,1,0:T(8,128)S(1)}, f32[1,128]{1,0:T(1,128)S(1)}) custom-call(f32[3,2,160,256]{3,2,1,0:T(8,128)} %now.1, f32[3,2,160,256]{3,2,1,0:T(8,128)} %before.1, f32[2,160,256]{2,1,0:T(8,128)} %lame.1, ...), custom_call_target="tpu_custom_call" | custom-call | tf_op jit(solution)/shard_map/leapfrog/pallas_call | solution.py:548
  56.8 1.2 %finish.1 = (f32[3,2,160,256]{3,2,1,0:T(8,128)}, f32[2,160,256]{2,1,0:T(8,128)}, f32[2,160,256]{2,1,0:T(8,128)}) custom-call(f32[3,2,2,160,128]{4,3,2,1,0:T(8,128)S(1)} %get-tuple-element.8.final, f32[2,2,160,128]{3,2,1,0:T(8,128)S(1)} %get-tuple-element.9.grad, f32[4,2,2,160,128]{4,3,2,1,0:T(8,128)S(1)} %get-tuple-element.10.s_vec, ...), custom_call_target="tpu_custom_call" | custom-call | tf_op jit(solution)/shard_map/finish/pallas_call | solution.py:581

commit v7 on v5

--- a/solution.py
+++ b/solution.py
@@ -44,11 +44,12 @@
     link_peer = jnp.clip(me + 2 * core - 1, 0, count - 1)
 
     barrier = pltpu.get_barrier_semaphore()
-    pl.semaphore_signal(barrier, inc=1, device_id={"gz": pair_peer}, device_id_type=MESH)
 
     @pl.when(linked)
     def _():
         pl.semaphore_signal(barrier, inc=1, device_id={"gz": link_peer}, device_id_type=MESH)
+
+    pl.semaphore_signal(barrier, inc=1, device_id={"gz": pair_peer}, device_id_type=MESH)
 
     inner = pl.ds(PAD, nx)
 
@@ -445,9 +446,6 @@
             device_id_type=MESH,
         ).start()
 
-    wait_sent(nxt)
-    wait_sent(cur)
-
     others = rows.at[pl.ds(0, count - 1)]
     everyone = pltpu.make_async_remote_copy(
         src_ref=others,
@@ -457,9 +455,11 @@
         device_id={"gz": lax.rem(me + 1, count)},
         device_id_type=MESH,
     )
-    everyone.wait_send()
     everyone.wait_recv()
     total[...] = jnp.sum(rows[...], axis=0)
+    everyone.wait_send()
+    wait_sent(nxt)
+    wait_sent(cur)
 
 
 def finish(

time: 58.1 us -> 58.1 us (level)
  no operation moved by 1% of the time
where the time goes in v7:
time: 58.1 us; the launch traced here: 58 us
  Pallas kernels  57.3 us (99%)
  between operations  0.64 us (1%)
    pallas_call x1, Pallas kernels, on_device(): pl.pallas_call(kernel, out_shape=(jax.ShapeDtypeStruct((3, *plane), f32),...  56.2 us
    pallas_call x1, Pallas kernels, on_device(): pl.pallas_call(finish, out_shape=(jax.ShapeDtypeStruct(now.shape, f32), j...  1.18 us

profile of v7, /device:TPU:1, one launch (start us, length us, event | category | flops | bytes accessed | tf_op | source)
XLA Modules:
  0.0 58.0 jit_solution(9437673085355692082)
XLA Ops:
  0.6 56.2 %leapfrog.1 = (f32[3,2,2,160,128]{4,3,2,1,0:T(8,128)S(1)}, f32[2,2,160,128]{3,2,1,0:T(8,128)S(1)}, f32[4,2,2,160,128]{4,3,2,1,0:T(8,128)S(1)}, f32[4,2,2,160,128]{4,3,2,1,0:T(8,128)S(1)}, f32[1,128]{1,0:T(1,128)S(1)}) custom-call(f32[3,2,160,256]{3,2,1,0:T(8,128)} %now.1, f32[3,2,160,256]{3,2,1,0:T(8,128)} %before.1, f32[2,160,256]{2,1,0:T(8,128)} %lame.1, ...), custom_call_target="tpu_custom_call" | custom-call | tf_op jit(solution)/shard_map/leapfrog/pallas_call | solution.py:545
  56.8 1.2 %finish.1 = (f32[3,2,160,256]{3,2,1,0:T(8,128)}, f32[2,160,256]{2,1,0:T(8,128)}, f32[2,160,256]{2,1,0:T(8,128)}) custom-call(f32[3,2,2,160,128]{4,3,2,1,0:T(8,128)S(1)} %get-tuple-element.8.final, f32[2,2,160,128]{3,2,1,0:T(8,128)S(1)} %get-tuple-element.9.grad, f32[4,2,2,160,128]{4,3,2,1,0:T(8,128)S(1)} %get-tuple-element.10.s_vec, ...), custom_call_target="tpu_custom_call" | custom-call | tf_op jit(solution)/shard_map/finish/pallas_call | solution.py:578
